TPU v7x, 32 devices: a whole 2x2x4 slice. The times are simulated.
32 devices in a mesh: groups: 2 (over y), seq: 16 (over z, x, core).
Axes of the slice: x: 2, y: 2, z: 4, core: 2. Of those that a mesh axis runs over, the one named last changes fastest.
Arguments:
- queries: bfloat16 [8192, 2048], P(('groups', 'seq')), parts along dimension 0, may hold values from -20 to 20
- keys: bfloat16 [8192, 2048], P(('groups', 'seq')), parts along dimension 0, may hold values from -20 to 20
- values: bfloat16 [8192, 2048], P(('groups', 'seq')), parts along dimension 0, may hold values from -6 to 6
- block_counts: int32 [16], P('groups'), parts along dimension 0, may hold values from 2 to 6, as said below
- last_tokens: int32 [32], P('groups'), parts along dimension 0, may hold values from 64 to 128
- pack_order: int32 [32], P('groups'), parts along dimension 0, may hold values from 0 to 15, as said below
- decode_slot: int32 [16], P('groups'), parts along dimension 0, may hold values from 0 to 7, each once
Outputs:
- attended: bfloat16 [8192, 2048], P(('groups', 'seq')), parts along dimension 0
- cache_keys: bfloat16 [32, 32, 128, 128], P(('groups', 'seq')), parts along dimension 0
- cache_values: bfloat16 [32, 32, 128, 128], P(('groups', 'seq')), parts along dimension 0
There are 2 independent parts, one for each index of `groups`. A program takes and returns all parts, laid end to end along the dimension named above; each array names one. Nothing has to cross between parts.
Inputs may be any that keep to these rules, and one draw needn't show every extreme that they name: `block_counts`: they sum to 24; the largest equals 6. `pack_order`: each prompt number appears once. The last 1 positions hold null prompts, and the position before them a conditional prompt of 6 blocks. `decode_slot`: each slot appears once.
All inputs are finite; a program needn't handle non-finite values.
Results may differ from a plain program's by a relative error of at most 0.0034.
Values may be sent and summed in bfloat16 or wider, within the bound.
A program may use at most 64 MiB of HBM per device.

v0:
```python
import jax
import jax.numpy as jnp
from jax import lax
from jax.sharding import PartitionSpec as P

HEADS = 16
HEAD_DIM = 128
BLOCK = 128
MAXB = 6
MASKED_SCORE = -1e30


def shifted(block, axis, distance):
    devices = range(lax.axis_size(axis))
    route = [(i - distance, i) for i in devices if i - distance in devices]
    return lax.ppermute(block, axis, route)


def block_tables(block_counts, last_tokens, pack_order, decode_slot, total_blocks, block):
    pair_count = block_counts.shape[0]
    prompts = 2 * pair_count
    prompt_ids = jnp.arange(prompts, dtype=jnp.int32)
    prompt_sizes = jnp.concatenate([block_counts, jnp.ones((pair_count,), jnp.int32)])
    picked = (pack_order[:, None] == prompt_ids[None, :]).astype(jnp.int32)
    packed_sizes = jnp.sum(picked * prompt_sizes[None, :], axis=1)
    packed_tails = jnp.sum(picked * last_tokens[None, :], axis=1)
    block_ends = jnp.cumsum(packed_sizes)
    starts = block_ends - packed_sizes
    blocks = jnp.arange(total_blocks, dtype=jnp.int32)
    member = (
        (starts[None, :] <= blocks[:, None]) & (blocks[:, None] < block_ends[None, :])
    ).astype(jnp.int32)
    position = jnp.sum(member * prompt_ids[None, :], axis=1)
    prompt = jnp.sum(member * pack_order[None, :], axis=1)
    within = blocks - jnp.sum(member * starts[None, :], axis=1)
    is_last = blocks + 1 == jnp.sum(member * block_ends[None, :], axis=1)
    valid_tokens = jnp.where(is_last, jnp.sum(member * packed_tails[None, :], axis=1), block)
    pair_ids = jnp.arange(pair_count, dtype=jnp.int32)
    earlier = (decode_slot[None, :] < decode_slot[:, None]).astype(jnp.int32)
    slot_start = jnp.sum(earlier * (block_counts + 1)[None, :], axis=1)
    pair_of = prompt % pair_count
    owner = (pair_of[:, None] == pair_ids[None, :]).astype(jnp.int32)
    base_slot = jnp.sum(owner * slot_start[None, :], axis=1)
    own_count = jnp.sum(owner * block_counts[None, :], axis=1)
    destination = base_slot + jnp.where(prompt >= pair_count, own_count, within)
    hits = (destination[None, :] == blocks[:, None]).astype(jnp.int32)
    source = jnp.sum(hits * blocks[None, :], axis=1)
    return (position, valid_tokens, source)


def hand_off(paired, source, devices):
    tokens_here = paired.shape[1]
    blocks_here = tokens_here // BLOCK
    splits = devices // HEADS
    slice_len = BLOCK // splits
    outgoing = paired.reshape(2, blocks_here, splits, slice_len, HEADS, HEAD_DIM)
    outgoing = jnp.transpose(outgoing, (4, 2, 0, 1, 3, 5)).reshape(
        devices, 2, blocks_here, slice_len, HEAD_DIM
    )
    arrived = lax.all_to_all(outgoing, "seq", split_axis=0, concat_axis=2, tiled=True)
    ordered = jnp.take(arrived[0], source, axis=1)
    return (ordered[0][None], ordered[1][None])


def attend(queries, paired, position, valid_tokens, own_index, reach):
    tokens_here, features = queries.shape
    blocks_here = tokens_here // BLOCK
    pieces = [paired]
    current = paired
    for distance in range(reach):
        current = shifted(current, "seq", 1)
        pieces.insert(0, current)
    prior_count = reach * blocks_here
    window = jnp.concatenate(pieces, axis=1)
    window_blocks = prior_count + blocks_here
    lead_blocks = reach * blocks_here
    padded_docs = jnp.concatenate([jnp.full((lead_blocks,), -1, jnp.int32), position])
    padded_valid = jnp.concatenate([jnp.zeros((lead_blocks,), jnp.int32), valid_tokens])
    first_block = own_index * blocks_here + lead_blocks - prior_count
    window_docs = lax.dynamic_slice_in_dim(padded_docs, first_block, window_blocks)
    window_valid = lax.dynamic_slice_in_dim(padded_valid, first_block, window_blocks)
    own_first = own_index * blocks_here
    query_docs = lax.dynamic_slice_in_dim(position, own_first, blocks_here)
    query_valid = lax.dynamic_slice_in_dim(valid_tokens, own_first, blocks_here)
    token_ids = jnp.arange(BLOCK, dtype=jnp.int32)
    key_docs = jnp.repeat(window_docs, BLOCK)
    key_limit = jnp.repeat(window_valid, BLOCK)
    key_tokens = jnp.tile(token_ids, window_blocks)
    key_order = jnp.arange(window_blocks * BLOCK, dtype=jnp.int32) - prior_count * BLOCK
    query_order = jnp.arange(tokens_here, dtype=jnp.int32)
    allowed = key_docs[None, :] == jnp.repeat(query_docs, BLOCK)[:, None]
    allowed = (
        allowed & (key_order[None, :] <= query_order[:, None]) & (key_tokens < key_limit)[None, :]
    )
    query_ok = jnp.tile(token_ids, blocks_here) < jnp.repeat(query_valid, BLOCK)
    score_scale = HEAD_DIM ** (-0.5)
    query_heads = jnp.moveaxis(queries.reshape(tokens_here, HEADS, HEAD_DIM), 1, 0)
    key_heads = jnp.moveaxis(window[0].reshape(-1, HEADS, HEAD_DIM), 1, 0)
    value_heads = jnp.moveaxis(window[1].reshape(-1, HEADS, HEAD_DIM), 1, 0)

    def one_head(operands):
        query_part, key_part, value_part = operands
        scores = (
            jnp.einsum("qd,kd->qk", query_part, key_part, preferred_element_type=jnp.float32)
            * score_scale
        )
        scores = jnp.where(allowed, scores, MASKED_SCORE)
        peak = jnp.max(scores, axis=1, keepdims=True)
        weights = jnp.exp(scores - peak)
        totals = jnp.sum(weights, axis=1, keepdims=True)
        mixed = jnp.dot(
            weights.astype(jnp.bfloat16), value_part, preferred_element_type=jnp.float32
        )
        return mixed / totals

    head_outputs = lax.map(one_head, (query_heads, key_heads, value_heads))
    merged = jnp.moveaxis(head_outputs, 0, 1).reshape(tokens_here, features)
    return jnp.where(query_ok[:, None], merged, 0.0).astype(jnp.bfloat16)


def local(queries, keys, values, block_counts, last_tokens, pack_order, decode_slot):
    devices = lax.axis_size("seq")
    own_index = lax.axis_index("seq")
    tokens_here = queries.shape[0]
    blocks_here = tokens_here // BLOCK
    reach = (MAXB + blocks_here - 2) // blocks_here
    position, valid_tokens, source = block_tables(
        block_counts, last_tokens, pack_order, decode_slot, blocks_here * devices, BLOCK
    )
    paired = jnp.stack([keys, values])
    attended = attend(queries, paired, position, valid_tokens, own_index, reach)
    cache_keys, cache_values = hand_off(paired, source, devices)
    return (attended, cache_keys, cache_values)


def solution(mesh):
    placed = (
        P(("groups", "seq"), None),
        P(("groups", "seq"), None),
        P(("groups", "seq"), None),
        P("groups"),
        P("groups"),
        P("groups"),
        P("groups"),
    )
    return jax.shard_map(
        local,
        mesh=mesh,
        in_specs=placed,
        out_specs=(
            P(("groups", "seq"), None),
            P(("groups", "seq"), None, None, None),
            P(("groups", "seq"), None, None, None),
        ),
        check_vma=False,
    )
```

profile of v0, /device:TPU:20, one launch (start us, length us, event | category | flops | bytes accessed | tf_op | source)
XLA Modules:
  0.0 189.0 jit_solution(15952049757768567406)
XLA Ops:
  0.6 1.6 copy.47
  2.8 1.5 pad_maximum_fusion
  4.2 1.9 %collective-permute-start = (bf16[2,256,2048]{1,2,0:T(8,128)(2,1)}, bf16[2,256,2048]{1,2,0:T(8,128)(2,1)}, u32[]{:S(2)}, u32[]{:S(2)}) collective-permute-start(bf16[2,256,2048]{1,2,0:T(8,128)(2,1)} %pad_maximum_fusion), channel_id=1, source_target_pairs={{0,1},{1,2},{2,3},{3,4},{4,5},{5,6},{6,7},{7,8},{8,9},{9,10},{10,1... | collective-permute-start | bytes 6291464 | tf_op jit(solution)/shard_map/ppermute | solution.py:16
  6.8 1.9 %copy.53 = bf16[16,2,2,128,128]{4,3,2,1,0:T(8,128)(2,1)} copy(bf16[16,2,2,128,128]{4,0,3,2,1:T(8,128)(2,1)S(1)} %maximum_bitcast_fusion) | data formatting | bytes 4194304 | tf_op jit(solution)/shard_map/reshape | solution.py:57
  8.8 6.6 %all-to-all-start = ((bf16[16,2,2,128,128]{4,3,2,1,0:T(8,128)(2,1)}), bf16[16,2,2,128,128]{4,3,2,1,0:T(8,128)(2,1)}, u32[]{:S(2)}, u32[]{:S(2)}) async-start(bf16[16,2,2,128,128]{4,3,2,1,0:T(8,128)(2,1)} %copy.53), calls=%async_computation | async-start | bytes 4194304 | tf_op jit(solution)/shard_map/all_to_all | solution.py:60
  15.4 51.1 %collective-permute-done = bf16[2,256,2048]{1,2,0:T(8,128)(2,1)} collective-permute-done((bf16[2,256,2048]{1,2,0:T(8,128)(2,1)}, bf16[2,256,2048]{1,2,0:T(8,128)(2,1)}, u32[]{:S(2)}, u32[]{:S(2)}) %collective-permute-start) | collective-permute-done | bytes 2097184 | tf_op jit(solution)/shard_map/ppermute | solution.py:16
  66.5 1.9 %collective-permute-start.1 = (bf16[2,256,2048]{1,2,0:T(8,128)(2,1)}, bf16[2,256,2048]{1,2,0:T(8,128)(2,1)}, u32[]{:S(2)}, u32[]{:S(2)}) collective-permute-start(bf16[2,256,2048]{1,2,0:T(8,128)(2,1)} %collective-permute-done), channel_id=1, source_target_pairs={{0,1},{1,2},{2,3},{3,4},{4,5},{5,6},{6,7},{7,8},{8,9},{9,10},{10,1... | collective-permute-start | bytes 6291464 | tf_op jit(solution)/shard_map/ppermute | solution.py:16
  69.5 30.8 %collective-permute-done.1 = bf16[2,256,2048]{1,2,0:T(8,128)(2,1)} collective-permute-done((bf16[2,256,2048]{1,2,0:T(8,128)(2,1)}, bf16[2,256,2048]{1,2,0:T(8,128)(2,1)}, u32[]{:S(2)}, u32[]{:S(2)}) %collective-permute-start.1) | collective-permute-done | bytes 2097184 | tf_op jit(solution)/shard_map/ppermute | solution.py:16
  100.3 1.9 %collective-permute-start.2 = (bf16[2,256,2048]{1,2,0:T(8,128)(2,1)}, bf16[2,256,2048]{1,2,0:T(8,128)(2,1)}, u32[]{:S(2)}, u32[]{:S(2)}) collective-permute-start(bf16[2,256,2048]{1,2,0:T(8,128)(2,1)} %collective-permute-done.1), channel_id=1, source_target_pairs={{0,1},{1,2},{2,3},{3,4},{4,5},{5,6},{6,7},{7,8},{8,9},{9,10},{10,1... | collective-permute-start | bytes 6291464 | tf_op jit(solution)/shard_map/ppermute | solution.py:16
  102.5 2.3 %copy.46 = bf16[256,2048]{0,1:T(8,128)(2,1)} copy(bf16[256,2048]{1,0:T(8,128)(2,1)} %param.9) | data formatting | bytes 2097152 | tf_op args[0]
  105.0 3.2 %copy.54 = bf16[16,2,2,128,128]{4,3,2,0,1:T(8,128)(2,1)} copy(bf16[16,2,2,128,128]{4,3,2,1,0:T(8,128)(2,1)} %all-to-all-done) | data formatting | bytes 4194304 | tf_op jit(solution)/shard_map/all_to_all | solution.py:60
  108.3 3.7 %gather_fusion = bf16[32,2,128,128]{3,2,1,0:T(8,128)(2,1)} fusion(bf16[2,32,128,128]{3,2,1,0:T(8,128)(2,1)} %bitcast.87, s32[1024]{0:T(1024)S(1)} %pad_clamp_fusion), kind=kCustom, calls=%fused_computation | custom fusion | bytes 4194432 | tf_op jit(solution)/shard_map/jit(_take)/gather | solution.py:61
  112.0 1.8 select_bitcast_fusion
  113.9 1.5 slice_bitcast_fusion
  115.3 13.6 %collective-permute-done.2 = bf16[2,256,2048]{1,2,0:T(8,128)(2,1)} collective-permute-done((bf16[2,256,2048]{1,2,0:T(8,128)(2,1)}, bf16[2,256,2048]{1,2,0:T(8,128)(2,1)}, u32[]{:S(2)}, u32[]{:S(2)}) %collective-permute-start.2) | collective-permute-done | bytes 2097184 | tf_op jit(solution)/shard_map/ppermute | solution.py:16
  128.9 3.9 %maximum_maximum_fusion = bf16[2,1024,2048]{1,2,0:T(8,128)(2,1)S(1)} fusion(bf16[1,256,2048]{1,2,0:T(8,128)(2,1)S(1)} %bitcast.86, bf16[1,256,2048]{1,2,0:T(8,128)(2,1)S(1)} %bitcast.84, bf16[2,256,2048]{1,2,0:T(8,128)(2,1)} %collective-permute-done, bf16[2,256,2048]{1,2,0:T(8,128)(2,1)} %collective-permute-done.1, ...), kind=kLoop, calls=%fused_computation.22 | loop fusion | flops 41943040 | bytes 16777216 | tf_op jit(solution)/shard_map/concatenate | solution.py:74
  132.8 3.7 %fusion.26 = (bf16[1,1024,2048]{1,2,0:T(8,128)(2,1)}, bf16[1,1024,2048]{1,2,0:T(8,128)(2,1)}) fusion(bf16[2,1024,2048]{1,2,0:T(8,128)(2,1)S(1)} %maximum_maximum_fusion), kind=kLoop, calls=%fused_computation.69 | loop fusion | bytes 16777216 | tf_op jit(solution)/shard_map/slice | solution.py:99
  136.4 51.3 %while.11 = (s32[]{:T(128)}, bf16[16,256,128]{2,1,0:T(8,128)(2,1)S(1)}, bf16[16,256,128]{1,2,0:T(8,128)(2,1)}, bf16[16,1024,128]{1,2,0:T(8,128)(2,1)}, bf16[16,1...) while((s32[]{:T(128)}, ...), condition=%wide.region_9.10_spmd.clone, body=%wide.region_6.0_spmd.clone.sunk | while | flops 137133568 | bytes 3884133 | solution.py:116
  136.4 1.5 fusion.35
  138.3 1.3 fusion.37
  139.6 1.5 fusion.35
  141.5 1.3 fusion.37
  142.9 1.5 fusion.35
  144.7 1.3 fusion.37
  146.1 1.5 fusion.35
  147.9 1.3 fusion.37
  149.3 1.5 fusion.35
  151.1 1.3 fusion.37
  152.5 1.5 fusion.35
  154.3 1.3 fusion.37
  155.7 1.5 fusion.35
  157.5 1.3 fusion.37
  158.9 1.5 fusion.35
  160.8 1.3 fusion.37
  162.1 1.5 fusion.35
  164.0 1.3 fusion.37
  165.3 1.5 fusion.35
  167.2 1.3 fusion.37
  168.5 1.5 fusion.35
  170.4 1.3 fusion.37
  171.7 1.5 fusion.35
  173.6 1.3 fusion.37
  174.9 1.5 fusion.35
  176.8 1.3 fusion.37
  178.1 1.5 fusion.35
  180.0 1.3 fusion.37
  181.4 1.5 fusion.35
  184.6 1.5 fusion.35
  (62 shorter events, 11.5 us)
Async XLA Ops:
  0.6 1.6 copy-start.1
  2.8 3.4 %copy-start = (bf16[256,2048]{1,0:T(8,128)(2,1)S(1)}, bf16[256,2048]{1,0:T(8,128)(2,1)}, u32[]{:S(2)}) copy-start(bf16[256,2048]{1,0:T(8,128)(2,1)} %param.10) | copy-start | bytes 3145732
  4.2 62.3 %collective-permute-start = (bf16[2,256,2048]{1,2,0:T(8,128)(2,1)}, bf16[2,256,2048]{1,2,0:T(8,128)(2,1)}, u32[]{:S(2)}, u32[]{:S(2)}) collective-permute-start(bf16[2,256,2048]{1,2,0:T(8,128)(2,1)} %pad_maximum_fusion), channel_id=1, source_target_pairs={{0,1},{1,2},{2,3},{3,4},{4,5},{5,6},{6,7},{7,8},{8,9},{9,10},{10,1... | collective-permute-start | bytes 6291464 | tf_op jit(solution)/shard_map/ppermute | solution.py:16
  8.8 59.6 %copy-start.5 = (s32[8]{0:T(128)S(1)}, s32[8]{0:T(128)}, u32[]{:S(2)}) copy-start(s32[8]{0:T(128)} %param.12) | copy-start | bytes 100
  8.8 59.7 %copy-start.2 = (s32[16]{0:T(128)S(1)}, s32[16]{0:T(128)}, u32[]{:S(2)}) copy-start(s32[16]{0:T(128)} %param.14) | copy-start | bytes 196
  8.8 59.7 %copy-start.4 = (s32[16]{0:T(128)S(1)}, s32[16]{0:T(128)}, u32[]{:S(2)}) copy-start(s32[16]{0:T(128)} %param.13) | copy-start | bytes 196
  8.8 60.3 %copy-start.3 = (s32[8]{0:T(128)S(1)}, s32[8]{0:T(128)}, u32[]{:S(2)}) copy-start(s32[8]{0:T(128)} %param.15) | copy-start | bytes 100
  8.8 96.2 %all-to-all-start = ((bf16[16,2,2,128,128]{4,3,2,1,0:T(8,128)(2,1)}), bf16[16,2,2,128,128]{4,3,2,1,0:T(8,128)(2,1)}, u32[]{:S(2)}, u32[]{:S(2)}) async-start(bf16[16,2,2,128,128]{4,3,2,1,0:T(8,128)(2,1)} %copy.53), calls=%async_computation | async-start | bytes 4194304 | tf_op jit(solution)/shard_map/all_to_all | solution.py:60
  66.5 33.8 %collective-permute-start.1 = (bf16[2,256,2048]{1,2,0:T(8,128)(2,1)}, bf16[2,256,2048]{1,2,0:T(8,128)(2,1)}, u32[]{:S(2)}, u32[]{:S(2)}) collective-permute-start(bf16[2,256,2048]{1,2,0:T(8,128)(2,1)} %collective-permute-done), channel_id=1, source_target_pairs={{0,1},{1,2},{2,3},{3,4},{4,5},{5,6},{6,7},{7,8},{8,9},{9,10},{10,1... | collective-permute-start | bytes 6291464 | tf_op jit(solution)/shard_map/ppermute | solution.py:16
  100.3 28.6 %collective-permute-start.2 = (bf16[2,256,2048]{1,2,0:T(8,128)(2,1)}, bf16[2,256,2048]{1,2,0:T(8,128)(2,1)}, u32[]{:S(2)}, u32[]{:S(2)}) collective-permute-start(bf16[2,256,2048]{1,2,0:T(8,128)(2,1)} %collective-permute-done.1), channel_id=1, source_target_pairs={{0,1},{1,2},{2,3},{3,4},{4,5},{5,6},{6,7},{7,8},{8,9},{9,10},{10,1... | collective-permute-start | bytes 6291464 | tf_op jit(solution)/shard_map/ppermute | solution.py:16
where the time goes:
time: 190 us; the launch traced here: 189 us
  waiting for transfers between devices  95.5 us (50%)
  matrix products  46.1 us (24%)
  local copies, waits for them, and re-layouts  19.4 us (10%)
  other arithmetic  14.5 us (8%)
  starting transfers between devices  12.3 us (6%)
    ppermute x3, waiting for transfers between devices, shifted(): return lax.ppermute(block, axis, route)  95.5 us
    dot_general x16, matrix products, one_head(): jnp.einsum('qd,kd->qk', query_part, key_part, preferred_element_type=jnp....  24.7 us
    dot_general x16, matrix products, one_head(): jnp.dot(weights.astype(jnp.bfloat16), value_part, preferred_element_type=...  21.4 us
    all_to_all x1, starting transfers between devices, hand_off(): lax.all_to_all(outgoing, 'seq', split_axis=0, concat_axis=2, tiled=True)  6.57 us
    unnamed x18, local copies, waits for them, and re-layouts  6.28 us
    ppermute x3, starting transfers between devices, shifted(): return lax.ppermute(block, axis, route)  5.73 us
    reduce_sum x16, other arithmetic, one_head(): totals = jnp.sum(weights, axis=1, keepdims=True)  4.88 us
    concatenate x1, other arithmetic, attend(): window = jnp.concatenate(pieces, axis=1)  3.88 us
  transfers between devices with their start and end apart: 4, of which 3 were waited for; matrix products, arithmetic and copies ran while one was open for 9% of the time, Pallas kernels for 0%

commit v1 on v0

--- a/solution.py
+++ b/solution.py
@@ -57,7 +57,19 @@
     outgoing = jnp.transpose(outgoing, (4, 2, 0, 1, 3, 5)).reshape(
         devices, 2, blocks_here, slice_len, HEAD_DIM
     )
-    arrived = lax.all_to_all(outgoing, "seq", split_axis=0, concat_axis=2, tiled=True)
+    ways, here = (lax.axis_size("seq"), lax.axis_index("seq"))
+    width = outgoing.shape[0] // ways
+    lengths = list(outgoing.shape)
+    lengths[0] = width
+    height = lengths[2]
+    lengths[2] = height * ways
+    full = jnp.zeros(lengths, outgoing.dtype)
+    for mask in range(ways):
+        part = lax.dynamic_slice_in_dim(outgoing, (here ^ mask) * width, width, axis=0)
+        if mask:
+            part = lax.ppermute(part, "seq", [(d, d ^ mask) for d in range(ways)])
+        full = lax.dynamic_update_slice_in_dim(full, part, (here ^ mask) * height, axis=2)
+    arrived = full
     ordered = jnp.take(arrived[0], source, axis=1)
     return (ordered[0][None], ordered[1][None])
 

time: 190 us -> 203 us (1.068)
  waiting for transfers between devices: 95.5 us -> 55.6 us
  starting transfers between devices: 12.3 us -> 41.6 us
  local copies, waits for them, and re-layouts: 19.4 us -> 39.4 us
  other arithmetic: 14.5 us -> 16.9 us
    ppermute x3, waiting for transfers between devices: 95.5 us -> 7.86 us  [shifted(): return lax.ppermute(block, axis, route)]
    ppermute x0 -> x15, waiting for transfers between devices: none -> 47.8 us  [hand_off(): part = lax.ppermute(part, 'seq', [(d, d ^ mask) for d in range(ways)])]
    ppermute x0 -> x15, starting transfers between devices: none -> 34.1 us  [hand_off(): part = lax.ppermute(part, 'seq', [(d, d ^ mask) for d in range(ways)])]
    unnamed x18 -> x66, local copies, waits for them, and re-layouts: 6.28 us -> 21.7 us
    all_to_all x1 -> x0, starting transfers between devices: 6.57 us -> none  [hand_off(): lax.all_to_all(outgoing, 'seq', split_axis=0, concat_axis=2, tiled=True)]
    another operation x1 -> x3, local copies, waits for them, and re-layouts: 0.09 us -> 5.84 us
    dynamic_update_slice x0 -> x16, local copies, waits for them, and re-layouts: none -> 3.94 us  [hand_off(): lax.dynamic_update_slice_in_dim(full, part, (here ^ mask) * height, axis=2)]
    all_to_all x1 -> x0, local copies, waits for them, and re-layouts: 3.23 us -> none  [hand_off(): lax.all_to_all(outgoing, 'seq', split_axis=0, concat_axis=2, tiled=True)]
  transfers between devices with their start and end apart: 4 -> 18, of which waited for: 3 -> 7; matrix products, arithmetic and copies ran while one was open for 9% -> 19% of each run, Pallas kernels for 0% -> 0%
where the time goes in v1:
time: 203 us; the launch traced here: 201 us
  waiting for transfers between devices  55.6 us (27%)
  matrix products  46.1 us (23%)
  starting transfers between devices  41.6 us (20%)
  local copies, waits for them, and re-layouts  39.4 us (19%)
  other arithmetic  16.9 us (8%)
    ppermute x15, waiting for transfers between devices, hand_off(): part = lax.ppermute(part, 'seq', [(d, d ^ mask) for d in range(ways)])  47.8 us
    ppermute x15, starting transfers between devices, hand_off(): part = lax.ppermute(part, 'seq', [(d, d ^ mask) for d in range(ways)])  34.1 us
    dot_general x16, matrix products, one_head(): jnp.einsum('qd,kd->qk', query_part, key_part, preferred_element_type=jnp....  24.7 us
    unnamed x66, local copies, waits for them, and re-layouts  21.7 us
    dot_general x16, matrix products, one_head(): jnp.dot(weights.astype(jnp.bfloat16), value_part, preferred_element_type=...  21.4 us
    ppermute x3, waiting for transfers between devices, shifted(): return lax.ppermute(block, axis, route)  7.86 us
    ppermute x3, starting transfers between devices, shifted(): return lax.ppermute(block, axis, route)  7.54 us
    another operation x2, local copies, waits for them, and re-layouts  5.59 us
  transfers between devices with their start and end apart: 18, of which 7 were waited for; matrix products, arithmetic and copies ran while one was open for 19% of the time, Pallas kernels for 0%

profile of v1, /device:TPU:20, one launch (start us, length us, event | category | flops | bytes accessed | tf_op | source)
XLA Modules:
  0.0 201.2 jit_solution(17770028794562548913)
XLA Ops:
  0.6 1.6 copy.35
  2.8 1.7 pad_maximum_fusion
  4.5 1.9 collective-permute-start
  8.3 5.5 %constant_dynamic-slice_fusion = (bf16[2,2,1,128,1,128]{5,4,3,1,2,0:T(2,128)(2,1)S(1)}, bf16[2,2,1,128,1,128]{5,4,3,1,2,0:T(2,128)(2,1)}, bf16[2,2,1,128,1,128]{...) fusion(bf16[2,2,1,128,16,128]{5,4,3,1,2,0:T(8,128)(2,1)S(1)} %c, ...), kind=kLoop, calls=%fused_computation.71 | loop fusion | bytes 4194368 | tf_op jit(solution)/shard_map/dynamic-slice.31
  14.5 1.6 collective-permute-start.3
  16.8 1.5 collective-permute-start.4
  19.0 1.4 collective-permute-start.6
  25.3 7.9 %collective-permute-done = bf16[2,256,2048]{1,2,0:T(8,128)(2,1)} collective-permute-done((bf16[2,256,2048]{1,2,0:T(8,128)(2,1)}, bf16[2,256,2048]{1,2,0:T(8,128)(2,1)}, u32[]{:S(2)}, u32[]{:S(2)}) %collective-permute-start) | collective-permute-done | bytes 2097184 | tf_op jit(solution)/shard_map/ppermute | solution.py:16
  33.2 2.8 %collective-permute-start.1 = (bf16[2,256,2048]{1,2,0:T(8,128)(2,1)}, bf16[2,256,2048]{1,2,0:T(8,128)(2,1)}, u32[]{:S(2)}, u32[]{:S(2)}) collective-permute-start(bf16[2,256,2048]{1,2,0:T(8,128)(2,1)} %collective-permute-done), channel_id=1, source_target_pairs={{0,1},{1,2},{2,3},{3,4},{4,5},{5,6},{6,7},{7,8},{8,9},{9,10},{10,1... | collective-permute-start | bytes 6291464 | tf_op jit(solution)/shard_map/ppermute | solution.py:16
  36.1 2.2 %copy.33 = bf16[256,2048]{0,1:T(8,128)(2,1)} copy(bf16[256,2048]{1,0:T(8,128)(2,1)} %param.9) | data formatting | bytes 2097152 | tf_op args[0]
  38.4 1.7 copy.91
  40.1 1.6 copy.90
  41.8 1.6 copy.89
  43.4 1.6 copy.88
  45.0 1.6 copy.87
  51.4 3.7 %collective-permute-start.7 = (bf16[1,2,2,128,128]{4,3,2,1,0:T(8,128)(2,1)}, bf16[1,2,2,128,128]{4,3,2,1,0:T(8,128)(2,1)S(1)}, u32[]{:S(2)}, u32[]{:S(2)}) collective-permute-start(bf16[1,2,2,128,128]{4,3,2,1,0:T(8,128)(2,1)} %bitcast.173), channel_id=1, source_target_pairs={{0,5},{1,4},{2,7},{3,6},{4,1},{5,0},{6,3},{7,2},{8,13},{9,12},{10,... | collective-permute-start | bytes 393224 | tf_op jit(solution)/shard_map/ppermute | solution.py:70
  60.4 3.9 %collective-permute-start.11 = (bf16[1,2,2,128,128]{4,3,2,1,0:T(8,128)(2,1)}, bf16[1,2,2,128,128]{4,3,2,1,0:T(8,128)(2,1)S(1)}, u32[]{:S(2)}, u32[]{:S(2)}) collective-permute-start(bf16[1,2,2,128,128]{4,3,2,1,0:T(8,128)(2,1)} %bitcast.169), channel_id=1, source_target_pairs={{0,9},{1,8},{2,11},{3,10},{4,13},{5,12},{6,15},{7,14},{8,1},{9,0},... | collective-permute-start | bytes 393224 | tf_op jit(solution)/shard_map/ppermute | solution.py:70
  65.1 8.2 %collective-permute-start.12 = (bf16[1,2,2,128,128]{4,3,2,1,0:T(8,128)(2,1)}, bf16[1,2,2,128,128]{4,3,2,1,0:T(8,128)(2,1)S(1)}, u32[]{:S(2)}, u32[]{:S(2)}) collective-permute-start(bf16[1,2,2,128,128]{4,3,2,1,0:T(8,128)(2,1)} %bitcast.168), channel_id=1, source_target_pairs={{0,10},{1,11},{2,8},{3,9},{4,14},{5,15},{6,12},{7,13},{8,2},{9,3},... | collective-permute-start | bytes 393224 | tf_op jit(solution)/shard_map/ppermute | solution.py:70
  73.5 1.5 collective-permute-start.14
  75.5 2.8 %collective-permute-start.2 = (bf16[2,256,2048]{1,2,0:T(8,128)(2,1)}, bf16[2,256,2048]{1,2,0:T(8,128)(2,1)}, u32[]{:S(2)}, u32[]{:S(2)}) collective-permute-start(bf16[2,256,2048]{1,2,0:T(8,128)(2,1)} %collective-permute-done.1), channel_id=1, source_target_pairs={{0,1},{1,2},{2,3},{3,4},{4,5},{5,6},{6,7},{7,8},{8,9},{9,10},{10,1... | collective-permute-start | bytes 6291464 | tf_op jit(solution)/shard_map/ppermute | solution.py:16
  78.3 7.6 %collective-permute-done.12 = bf16[1,2,2,128,128]{4,3,2,1,0:T(8,128)(2,1)S(1)} collective-permute-done((bf16[1,2,2,128,128]{4,3,2,1,0:T(8,128)(2,1)}, bf16[1,2,2,128,128]{4,3,2,1,0:T(8,128)(2,1)S(1)}, u32[]{:S(2)}, u32[]{:S(2)}) %collective-permute-start.12) | collective-permute-done | bytes 131104 | tf_op jit(solution)/shard_map/ppermute | solution.py:70
  86.0 4.1 %collective-permute-start.16 = (bf16[1,2,2,128,128]{4,3,2,1,0:T(8,128)(2,1)S(1)}, bf16[1,2,2,128,128]{4,3,2,1,0:T(8,128)(2,1)S(1)}, u32[]{:S(2)}, u32[]{:S(2)}) collective-permute-start(bf16[1,2,2,128,128]{4,3,2,1,0:T(8,128)(2,1)S(1)} %bitcast.164), channel_id=1, source_target_pairs={{0,14},{1,15},{2,12},{3,13},{4,10},{5,11},{6,8},{7,9},{8,6},{9,7},... | collective-permute-start | bytes 393224 | tf_op jit(solution)/shard_map/ppermute | solution.py:70
  90.2 6.0 %collective-permute-start.17 = (bf16[1,2,2,128,128]{4,3,2,1,0:T(8,128)(2,1)S(1)}, bf16[1,2,2,128,128]{4,3,2,1,0:T(8,128)(2,1)S(1)}, u32[]{:S(2)}, u32[]{:S(2)}) collective-permute-start(bf16[1,2,2,128,128]{4,3,2,1,0:T(8,128)(2,1)S(1)} %bitcast.163), channel_id=1, source_target_pairs={{0,15},{1,14},{2,13},{3,12},{4,11},{5,10},{6,9},{7,8},{8,7},{9,6},... | collective-permute-start | bytes 393224 | tf_op jit(solution)/shard_map/ppermute | solution.py:70
  96.2 6.7 %collective-permute-done.15 = bf16[1,2,2,128,128]{4,3,2,1,0:T(8,128)(2,1)S(1)} collective-permute-done((bf16[1,2,2,128,128]{4,3,2,1,0:T(8,128)(2,1)S(1)}, bf16[1,2,2,128,128]{4,3,2,1,0:T(8,128)(2,1)S(1)}, u32[]{:S(2)}, u32[]{:S(2)}) %collective-permute-start.15) | collective-permute-done | bytes 131104 | tf_op jit(solution)/shard_map/ppermute | solution.py:70
  103.0 3.8 %collective-permute-done.16 = bf16[1,2,2,128,128]{4,3,2,1,0:T(8,128)(2,1)S(1)} collective-permute-done((bf16[1,2,2,128,128]{4,3,2,1,0:T(8,128)(2,1)S(1)}, bf16[1,2,2,128,128]{4,3,2,1,0:T(8,128)(2,1)S(1)}, u32[]{:S(2)}, u32[]{:S(2)}) %collective-permute-start.16) | collective-permute-done | bytes 131104 | tf_op jit(solution)/shard_map/ppermute | solution.py:70
  106.8 28.7 %collective-permute-done.17 = bf16[1,2,2,128,128]{4,3,2,1,0:T(8,128)(2,1)S(1)} collective-permute-done((bf16[1,2,2,128,128]{4,3,2,1,0:T(8,128)(2,1)S(1)}, bf16[1,2,2,128,128]{4,3,2,1,0:T(8,128)(2,1)S(1)}, u32[]{:S(2)}, u32[]{:S(2)}) %collective-permute-start.17) | collective-permute-done | bytes 131104 | tf_op jit(solution)/shard_map/ppermute | solution.py:70
  135.5 2.2 %gather_fusion = bf16[32,2,128,128]{3,2,1,0:T(8,128)(2,1)} fusion(bf16[2,32,128,128]{3,2,1,0:T(8,128)(2,1)S(1)} %bitcast_dynamic-update-slice_fusion.1, s32[1024]{0:T(1024)S(1)} %pad_clamp_fusion), kind=kCustom, calls=%fused_computation | custom fusion | bytes 4194432 | tf_op jit(solution)/shard_map/jit(_take)/gather | solution.py:73
  137.6 1.8 select_bitcast_fusion
  139.5 1.5 slice_bitcast_fusion
  141.1 3.9 %maximum_maximum_fusion = bf16[2,1024,2048]{1,2,0:T(8,128)(2,1)S(1)} fusion(bf16[1,256,2048]{1,2,0:T(8,128)(2,1)S(1)} %bitcast.152, bf16[1,256,2048]{1,2,0:T(8,128)(2,1)S(1)} %bitcast.154, bf16[2,256,2048]{1,2,0:T(8,128)(2,1)} %collective-permute-done, bf16[2,256,2048]{1,2,0:T(8,128)(2,1)} %collective-permute-done.1, ...), kind=kLoop, calls=%fused_computation.22 | loop fusion | flops 41943040 | bytes 16777216 | tf_op jit(solution)/shard_map/concatenate | solution.py:86
  145.0 3.7 %fusion.26 = (bf16[1,1024,2048]{1,2,0:T(8,128)(2,1)}, bf16[1,1024,2048]{1,2,0:T(8,128)(2,1)}) fusion(bf16[2,1024,2048]{1,2,0:T(8,128)(2,1)S(1)} %maximum_maximum_fusion), kind=kLoop, calls=%fused_computation.117 | loop fusion | bytes 16777216 | tf_op jit(solution)/shard_map/slice | solution.py:111
  148.7 51.3 %while.11 = (s32[]{:T(128)}, bf16[16,256,128]{2,1,0:T(8,128)(2,1)S(1)}, bf16[16,256,128]{1,2,0:T(8,128)(2,1)}, bf16[16,1024,128]{1,2,0:T(8,128)(2,1)}, bf16[16,1...) while((s32[]{:T(128)}, ...), condition=%wide.region_9.10_spmd.clone, body=%wide.region_6.0_spmd.clone.sunk | while | flops 137133568 | bytes 3884141 | solution.py:128
  148.7 1.5 fusion.35
  151.9 1.5 fusion.35
  155.1 1.5 fusion.35
  158.3 1.5 fusion.35
  161.5 1.5 fusion.35
  164.7 1.5 fusion.35
  167.9 1.5 fusion.35
  171.1 1.5 fusion.35
  174.3 1.5 fusion.35
  177.5 1.5 fusion.35
  180.7 1.5 fusion.35
  183.9 1.5 fusion.35
  187.2 1.5 fusion.35
  190.4 1.5 fusion.35
  193.6 1.5 fusion.35
  196.8 1.5 fusion.35
  (154 shorter events, 48.5 us)
Async XLA Ops:
  0.6 1.6 copy-start.2
  2.8 1.7 copy-start
  4.5 28.7 %collective-permute-start = (bf16[2,256,2048]{1,2,0:T(8,128)(2,1)}, bf16[2,256,2048]{1,2,0:T(8,128)(2,1)}, u32[]{:S(2)}, u32[]{:S(2)}) collective-permute-start(bf16[2,256,2048]{1,2,0:T(8,128)(2,1)} %pad_maximum_fusion), channel_id=1, source_target_pairs={{0,1},{1,2},{2,3},{3,4},{4,5},{5,6},{6,7},{7,8},{8,9},{9,10},{10,1... | collective-permute-start | bytes 6291464 | tf_op jit(solution)/shard_map/ppermute | solution.py:16
  6.5 1.2 copy-start.3
  8.3 12.2 %copy-start.18 = (s32[8]{0:T(128)S(1)}, s32[8]{0:T(128)}, u32[]{:S(2)}) copy-start(s32[8]{0:T(128)} %param.12) | copy-start | bytes 100
  8.3 12.2 %copy-start.14 = (s32[16]{0:T(128)S(1)}, s32[16]{0:T(128)}, u32[]{:S(2)}) copy-start(s32[16]{0:T(128)} %param.14) | copy-start | bytes 196
  8.3 12.2 %copy-start.17 = (s32[16]{0:T(128)S(1)}, s32[16]{0:T(128)}, u32[]{:S(2)}) copy-start(s32[16]{0:T(128)} %param.13) | copy-start | bytes 196
  8.3 13.6 %copy-start.15 = (s32[8]{0:T(128)S(1)}, s32[8]{0:T(128)}, u32[]{:S(2)}) copy-start(s32[8]{0:T(128)} %param.15) | copy-start | bytes 100
  14.5 36.9 %collective-permute-start.3 = (bf16[1,2,2,128,128]{4,3,2,1,0:T(8,128)(2,1)}, bf16[1,2,2,128,128]{4,3,2,1,0:T(8,128)(2,1)}, u32[]{:S(2)}, u32[]{:S(2)}) collective-permute-start(bf16[1,2,2,128,128]{4,3,2,1,0:T(8,128)(2,1)} %bitcast.142), channel_id=1, source_target_pairs={{0,1},{1,0},{2,3},{3,2},{4,5},{5,4},{6,7},{7,6},{8,9},{9,8},{10,11... | collective-permute-start | bytes 393224 | tf_op jit(solution)/shard_map/ppermute | solution.py:70
  16.8 39.2 %collective-permute-start.4 = (bf16[1,2,2,128,128]{4,3,2,1,0:T(8,128)(2,1)}, bf16[1,2,2,128,128]{4,3,2,1,0:T(8,128)(2,1)}, u32[]{:S(2)}, u32[]{:S(2)}) collective-permute-start(bf16[1,2,2,128,128]{4,3,2,1,0:T(8,128)(2,1)} %bitcast.141), channel_id=1, source_target_pairs={{0,2},{1,3},{2,0},{3,1},{4,6},{5,7},{6,4},{7,5},{8,10},{9,11},{10,... | collective-permute-start | bytes 393224 | tf_op jit(solution)/shard_map/ppermute | solution.py:70
  19.0 38.9 %collective-permute-start.5 = (bf16[1,2,2,128,128]{4,3,2,1,0:T(8,128)(2,1)}, bf16[1,2,2,128,128]{4,3,2,1,0:T(8,128)(2,1)}, u32[]{:S(2)}, u32[]{:S(2)}) collective-permute-start(bf16[1,2,2,128,128]{4,3,2,1,0:T(8,128)(2,1)} %bitcast.140), channel_id=1, source_target_pairs={{0,3},{1,2},{2,1},{3,0},{4,7},{5,6},{6,5},{7,4},{8,11},{9,10},{10,... | collective-permute-start | bytes 393224 | tf_op jit(solution)/shard_map/ppermute | solution.py:70
  19.0 40.0 %collective-permute-start.6 = (bf16[1,2,2,128,128]{4,3,2,1,0:T(8,128)(2,1)S(1)}, bf16[1,2,2,128,128]{4,3,2,1,0:T(8,128)(2,1)}, u32[]{:S(2)}, u32[]{:S(2)}) collective-permute-start(bf16[1,2,2,128,128]{4,3,2,1,0:T(8,128)(2,1)S(1)} %bitcast.162), channel_id=1, source_target_pairs={{0,4},{1,5},{2,6},{3,7},{4,0},{5,1},{6,2},{7,3},{8,12},{9,13},{10,... | collective-permute-start | bytes 393224 | tf_op jit(solution)/shard_map/ppermute | solution.py:70
  21.8 3.5 %copy-start.10 = (bf16[2,2,1,128,1,128]{5,4,3,1,2,0:T(2,128)(2,1)S(1)}, bf16[2,2,1,128,1,128]{5,4,3,1,2,0:T(2,128)(2,1)}, u32[]{:S(2)}) copy-start(bf16[2,2,1,128,1,128]{5,4,3,1,2,0:T(2,128)(2,1)} %get-tuple-element.144) | copy-start | bytes 393220
  21.8 14.2 %copy-start.21 = (s32[2]{0:T(128)S(1)}, s32[2]{0:T(128)}, u32[]{:S(2)}) copy-start(s32[2]{0:T(128)} %dynamic_slice.69) | copy-start | bytes 28
  33.2 42.3 %collective-permute-start.1 = (bf16[2,256,2048]{1,2,0:T(8,128)(2,1)}, bf16[2,256,2048]{1,2,0:T(8,128)(2,1)}, u32[]{:S(2)}, u32[]{:S(2)}) collective-permute-start(bf16[2,256,2048]{1,2,0:T(8,128)(2,1)} %collective-permute-done), channel_id=1, source_target_pairs={{0,1},{1,2},{2,3},{3,4},{4,5},{5,6},{6,7},{7,8},{8,9},{9,10},{10,1... | collective-permute-start | bytes 6291464 | tf_op jit(solution)/shard_map/ppermute | solution.py:16
  38.4 8.3 %copy-start.9 = (bf16[2,2,1,128,1,128]{5,4,3,1,2,0:T(2,128)(2,1)S(1)}, bf16[2,2,1,128,1,128]{5,4,3,1,2,0:T(2,128)(2,1)}, u32[]{:S(2)}) copy-start(bf16[2,2,1,128,1,128]{5,4,3,1,2,0:T(2,128)(2,1)} %get-tuple-element.134) | copy-start | bytes 393220
  38.4 8.9 %copy-start.8 = (bf16[2,2,1,128,1,128]{5,4,3,1,2,0:T(2,128)(2,1)S(1)}, bf16[2,2,1,128,1,128]{5,4,3,1,2,0:T(2,128)(2,1)}, u32[]{:S(2)}) copy-start(bf16[2,2,1,128,1,128]{5,4,3,1,2,0:T(2,128)(2,1)} %get-tuple-element.133) | copy-start | bytes 393220
  38.4 9.6 %copy-start.7 = (bf16[2,2,1,128,1,128]{5,4,3,1,2,0:T(2,128)(2,1)S(1)}, bf16[2,2,1,128,1,128]{5,4,3,1,2,0:T(2,128)(2,1)}, u32[]{:S(2)}) copy-start(bf16[2,2,1,128,1,128]{5,4,3,1,2,0:T(2,128)(2,1)} %get-tuple-element.132) | copy-start | bytes 393220
  38.4 10.3 %copy-start.6 = (bf16[2,2,1,128,1,128]{5,4,3,1,2,0:T(2,128)(2,1)S(1)}, bf16[2,2,1,128,1,128]{5,4,3,1,2,0:T(2,128)(2,1)}, u32[]{:S(2)}) copy-start(bf16[2,2,1,128,1,128]{5,4,3,1,2,0:T(2,128)(2,1)} %get-tuple-element.131) | copy-start | bytes 393220
  38.4 10.9 %copy-start.5 = (bf16[2,2,1,128,1,128]{5,4,3,1,2,0:T(2,128)(2,1)S(1)}, bf16[2,2,1,128,1,128]{5,4,3,1,2,0:T(2,128)(2,1)}, u32[]{:S(2)}) copy-start(bf16[2,2,1,128,1,128]{5,4,3,1,2,0:T(2,128)(2,1)} %get-tuple-element.130) | copy-start | bytes 393220
  50.7 35.3 %copy-start.12 = (bf16[2,2,1,128,1,128]{5,3,4,1,2,0:T(8,128)(2,1)S(1)}, bf16[2,2,1,128,1,128]{5,3,4,1,2,0:T(8,128)(2,1)}, u32[]{:S(2)}) copy-start(bf16[2,2,1,128,1,128]{5,3,4,1,2,0:T(8,128)(2,1)} %copy.82) | copy-start | bytes 393220
  50.7 39.5 %copy-start.11 = (bf16[2,2,1,128,1,128]{5,3,4,1,2,0:T(8,128)(2,1)S(1)}, bf16[2,2,1,128,1,128]{5,3,4,1,2,0:T(8,128)(2,1)}, u32[]{:S(2)}) copy-start(bf16[2,2,1,128,1,128]{5,3,4,1,2,0:T(8,128)(2,1)} %copy.81) | copy-start | bytes 393220
  50.7 24.3 %copy-start.13 = (bf16[2,2,1,128,1,128]{5,3,4,1,2,0:T(8,128)(2,1)S(1)}, bf16[2,2,1,128,1,128]{5,3,4,1,2,0:T(8,128)(2,1)}, u32[]{:S(2)}) copy-start(bf16[2,2,1,128,1,128]{5,3,4,1,2,0:T(8,128)(2,1)} %copy.83) | copy-start | bytes 393220
  51.4 9.0 %collective-permute-start.7 = (bf16[1,2,2,128,128]{4,3,2,1,0:T(8,128)(2,1)}, bf16[1,2,2,128,128]{4,3,2,1,0:T(8,128)(2,1)S(1)}, u32[]{:S(2)}, u32[]{:S(2)}) collective-permute-start(bf16[1,2,2,128,128]{4,3,2,1,0:T(8,128)(2,1)} %bitcast.173), channel_id=1, source_target_pairs={{0,5},{1,4},{2,7},{3,6},{4,1},{5,0},{6,3},{7,2},{8,13},{9,12},{10,... | collective-permute-start | bytes 393224 | tf_op jit(solution)/shard_map/ppermute | solution.py:70
  56.0 9.2 %collective-permute-start.8 = (bf16[1,2,2,128,128]{4,3,2,1,0:T(8,128)(2,1)}, bf16[1,2,2,128,128]{4,3,2,1,0:T(8,128)(2,1)S(1)}, u32[]{:S(2)}, u32[]{:S(2)}) collective-permute-start(bf16[1,2,2,128,128]{4,3,2,1,0:T(8,128)(2,1)} %bitcast.172), channel_id=1, source_target_pairs={{0,6},{1,7},{2,4},{3,5},{4,2},{5,3},{6,0},{7,1},{8,14},{9,15},{10,... | collective-permute-start | bytes 393224 | tf_op jit(solution)/shard_map/ppermute | solution.py:70
  57.9 15.4 %collective-permute-start.9 = (bf16[1,2,2,128,128]{4,3,2,1,0:T(8,128)(2,1)}, bf16[1,2,2,128,128]{4,3,2,1,0:T(8,128)(2,1)S(1)}, u32[]{:S(2)}, u32[]{:S(2)}) collective-permute-start(bf16[1,2,2,128,128]{4,3,2,1,0:T(8,128)(2,1)} %bitcast.171), channel_id=1, source_target_pairs={{0,7},{1,6},{2,5},{3,4},{4,3},{5,2},{6,1},{7,0},{8,15},{9,14},{10,... | collective-permute-start | bytes 393224 | tf_op jit(solution)/shard_map/ppermute | solution.py:70
  59.0 14.4 %collective-permute-start.10 = (bf16[1,2,2,128,128]{4,3,2,1,0:T(8,128)(2,1)}, bf16[1,2,2,128,128]{4,3,2,1,0:T(8,128)(2,1)S(1)}, u32[]{:S(2)}, u32[]{:S(2)}) collective-permute-start(bf16[1,2,2,128,128]{4,3,2,1,0:T(8,128)(2,1)} %bitcast.170), channel_id=1, source_target_pairs={{0,8},{1,9},{2,10},{3,11},{4,12},{5,13},{6,14},{7,15},{8,0},{9,1},... | collective-permute-start | bytes 393224 | tf_op jit(solution)/shard_map/ppermute | solution.py:70
  60.4 14.6 %collective-permute-start.11 = (bf16[1,2,2,128,128]{4,3,2,1,0:T(8,128)(2,1)}, bf16[1,2,2,128,128]{4,3,2,1,0:T(8,128)(2,1)S(1)}, u32[]{:S(2)}, u32[]{:S(2)}) collective-permute-start(bf16[1,2,2,128,128]{4,3,2,1,0:T(8,128)(2,1)} %bitcast.169), channel_id=1, source_target_pairs={{0,9},{1,8},{2,11},{3,10},{4,13},{5,12},{6,15},{7,14},{8,1},{9,0},... | collective-permute-start | bytes 393224 | tf_op jit(solution)/shard_map/ppermute | solution.py:70
  65.1 20.8 %collective-permute-start.12 = (bf16[1,2,2,128,128]{4,3,2,1,0:T(8,128)(2,1)}, bf16[1,2,2,128,128]{4,3,2,1,0:T(8,128)(2,1)S(1)}, u32[]{:S(2)}, u32[]{:S(2)}) collective-permute-start(bf16[1,2,2,128,128]{4,3,2,1,0:T(8,128)(2,1)} %bitcast.168), channel_id=1, source_target_pairs={{0,10},{1,11},{2,8},{3,9},{4,14},{5,15},{6,12},{7,13},{8,2},{9,3},... | collective-permute-start | bytes 393224 | tf_op jit(solution)/shard_map/ppermute | solution.py:70
  73.4 16.8 %collective-permute-start.13 = (bf16[1,2,2,128,128]{4,3,2,1,0:T(8,128)(2,1)}, bf16[1,2,2,128,128]{4,3,2,1,0:T(8,128)(2,1)S(1)}, u32[]{:S(2)}, u32[]{:S(2)}) collective-permute-start(bf16[1,2,2,128,128]{4,3,2,1,0:T(8,128)(2,1)} %bitcast.167), channel_id=1, source_target_pairs={{0,11},{1,10},{2,9},{3,8},{4,15},{5,14},{6,13},{7,12},{8,3},{9,2},... | collective-permute-start | bytes 393224 | tf_op jit(solution)/shard_map/ppermute | solution.py:70
  73.5 22.7 %collective-permute-start.14 = (bf16[1,2,2,128,128]{4,3,2,1,0:T(8,128)(2,1)}, bf16[1,2,2,128,128]{4,3,2,1,0:T(8,128)(2,1)S(1)}, u32[]{:S(2)}, u32[]{:S(2)}) collective-permute-start(bf16[1,2,2,128,128]{4,3,2,1,0:T(8,128)(2,1)} %bitcast.166), channel_id=1, source_target_pairs={{0,12},{1,13},{2,14},{3,15},{4,8},{5,9},{6,10},{7,11},{8,4},{9,5},... | collective-permute-start | bytes 393224 | tf_op jit(solution)/shard_map/ppermute | solution.py:70
  75.0 27.9 %collective-permute-start.15 = (bf16[1,2,2,128,128]{4,3,2,1,0:T(8,128)(2,1)S(1)}, bf16[1,2,2,128,128]{4,3,2,1,0:T(8,128)(2,1)S(1)}, u32[]{:S(2)}, u32[]{:S(2)}) collective-permute-start(bf16[1,2,2,128,128]{4,3,2,1,0:T(8,128)(2,1)S(1)} %bitcast.165), channel_id=1, source_target_pairs={{0,13},{1,12},{2,15},{3,14},{4,9},{5,8},{6,11},{7,10},{8,5},{9,4},... | collective-permute-start | bytes 393224 | tf_op jit(solution)/shard_map/ppermute | solution.py:70
  75.5 65.4 %collective-permute-start.2 = (bf16[2,256,2048]{1,2,0:T(8,128)(2,1)}, bf16[2,256,2048]{1,2,0:T(8,128)(2,1)}, u32[]{:S(2)}, u32[]{:S(2)}) collective-permute-start(bf16[2,256,2048]{1,2,0:T(8,128)(2,1)} %collective-permute-done.1), channel_id=1, source_target_pairs={{0,1},{1,2},{2,3},{3,4},{4,5},{5,6},{6,7},{7,8},{8,9},{9,10},{10,1... | collective-permute-start | bytes 6291464 | tf_op jit(solution)/shard_map/ppermute | solution.py:16
  86.0 20.8 %collective-permute-start.16 = (bf16[1,2,2,128,128]{4,3,2,1,0:T(8,128)(2,1)S(1)}, bf16[1,2,2,128,128]{4,3,2,1,0:T(8,128)(2,1)S(1)}, u32[]{:S(2)}, u32[]{:S(2)}) collective-permute-start(bf16[1,2,2,128,128]{4,3,2,1,0:T(8,128)(2,1)S(1)} %bitcast.164), channel_id=1, source_target_pairs={{0,14},{1,15},{2,12},{3,13},{4,10},{5,11},{6,8},{7,9},{8,6},{9,7},... | collective-permute-start | bytes 393224 | tf_op jit(solution)/shard_map/ppermute | solution.py:70
  90.2 45.2 %collective-permute-start.17 = (bf16[1,2,2,128,128]{4,3,2,1,0:T(8,128)(2,1)S(1)}, bf16[1,2,2,128,128]{4,3,2,1,0:T(8,128)(2,1)S(1)}, u32[]{:S(2)}, u32[]{:S(2)}) collective-permute-start(bf16[1,2,2,128,128]{4,3,2,1,0:T(8,128)(2,1)S(1)} %bitcast.163), channel_id=1, source_target_pairs={{0,15},{1,14},{2,13},{3,12},{4,11},{5,10},{6,9},{7,8},{8,7},{9,6},... | collective-permute-start | bytes 393224 | tf_op jit(solution)/shard_map/ppermute | solution.py:70
  135.4 2.2 %copy-start.16 = (pred[32]{0:T(512)(128)(4,1)S(1)}, pred[32]{0:T(512)(128)(4,1)}, u32[]{:S(2)}) copy-start(pred[32]{0:T(512)(128)(4,1)} %compare_and_fusion) | copy-start | bytes 100
  139.5 1.6 copy-start.1
  145.0 3.7 %copy-start.4 = (bf16[16,256,128]{2,1,0:T(8,128)(2,1)S(1)}, bf16[16,256,128]{2,1,0:T(8,128)(2,1)}, u32[]{:S(2)}) copy-start(bf16[16,256,128]{2,1,0:T(8,128)(2,1)} %custom-call.3) | copy-start | bytes 3145732
  145.0 3.7 %copy-start.19 = (s32[256]{0:T(256)S(1)}, s32[256]{0:T(256)}, u32[]{:S(2)}) copy-start(s32[256]{0:T(256)} %broadcast_bitcast_fusion.1) | copy-start | bytes 3076
  145.0 3.7 %copy-start.20 = (pred[1024]{0:T(1024)(128)(4,1)S(1)}, pred[1024]{0:T(1024)(128)(4,1)}, u32[]{:S(2)}) copy-start(pred[1024]{0:T(1024)(128)(4,1)} %fusion.21) | copy-start | bytes 3076
